TPU v7x, 32 devices: a whole 2x2x4 slice. The times are simulated.
32 devices in a mesh: emb: 4 (over x, core), heads: 8 (over z, y).
Axes of the slice: x: 2, y: 2, z: 4, core: 2. Of those that a mesh axis runs over, the one named last changes fastest.
Arguments:
- hidden_in: bfloat16 [16, 8192], P(None, 'emb'), may hold values from -6 to 6
- w_z: bfloat16 [8192, 16384], P('emb', 'heads'), may hold values from -0.0625 to 0.0625
- w_x: bfloat16 [8192, 16384], P('emb', 'heads'), may hold values from -0.0625 to 0.0625
- w_bc: bfloat16 [8192, 4096], P('emb'), may hold values from -0.0625 to 0.0625
- w_dt: bfloat16 [8192, 256], P('emb', 'heads'), may hold values from -0.0625 to 0.0625
- dt_bias: float32 [256], P('heads'), may hold values from -4 to -1
- a_log: float32 [256], P('heads'), may hold values from 0 to 2.77
- skip_gain: float32 [256], P('heads'), may hold values from 0.5 to 2
- conv_x: bfloat16 [16, 3, 16384], P('emb', None, 'heads'), may hold values from -6 to 6
- conv_bc: bfloat16 [16, 3, 4096], P('emb'), may hold values from -6 to 6
- conv_wx: float32 [4, 16384], P(None, 'heads'), may hold values from -3 to 3
- conv_wbc: float32 [4, 4096], replicated, may hold values from -3 to 3
- ssm_state: float32 [16, 256, 64, 256], P('emb', 'heads'), may hold values from -0.6 to 0.6
- norm_gain: float32 [16384], P('heads'), may hold values from 0.5 to 1.5
- w_out: bfloat16 [16384, 8192], P('heads', 'emb'), may hold values from -0.046875 to 0.046875
Outputs:
- mixed: bfloat16 [16, 8192], P(None, 'emb')
- new_state: float32 [16, 256, 64, 256], P('emb', 'heads')
All inputs are finite; a program needn't handle non-finite values.
Results may differ from a plain program's by a relative error of at most 0.0051.
Values may be sent and summed in bfloat16 or wider, within the bound.
A program may use at most 128 MiB of HBM per device.

v0:
```python
import jax
import jax.numpy as jnp
from jax import lax
from jax.sharding import PartitionSpec as P

H = 256
P_SIZE = 64
N = 256
G = 8


def from_partner(value, axis, apart):
    mask = 2**apart
    pairs = [(source, source ^ mask) for source in range(lax.axis_size(axis))]
    return lax.ppermute(value, axis, pairs)


def on_device(
    hidden_in,
    w_z,
    w_x,
    w_bc,
    w_dt,
    dt_bias,
    a_log,
    skip_gain,
    conv_x,
    conv_bc,
    conv_wx,
    conv_wbc,
    ssm_state,
    norm_gain,
    w_out,
):
    heads_dev = w_dt.shape[1]
    emb_rows = w_bc.shape[0]
    batch_dev = conv_x.shape[0]
    group_span = lax.axis_size("heads") // G
    my_group = lax.axis_index("heads") // group_span
    bc_cols = lax.dynamic_slice_in_dim(w_bc.reshape(emb_rows, 2, G, N), my_group, 1, 2).reshape(
        emb_rows, 2 * N
    )
    z_part = jnp.dot(hidden_in, w_z, preferred_element_type=jnp.float32)
    x_part = jnp.dot(hidden_in, w_x, preferred_element_type=jnp.float32)
    bc_part = jnp.dot(hidden_in, bc_cols, preferred_element_type=jnp.float32)
    dt_part = jnp.dot(hidden_in, w_dt, preferred_element_type=jnp.float32)
    summed_all = lax.psum((z_part, x_part, bc_part, dt_part), "emb")
    first_row = lax.axis_index("emb") * batch_dev
    z_pre = lax.dynamic_slice_in_dim(summed_all[0], first_row, batch_dev, 0)
    x_pre = lax.dynamic_slice_in_dim(summed_all[1], first_row, batch_dev, 0)
    bc_pre = lax.dynamic_slice_in_dim(summed_all[2], first_row, batch_dev, 0)
    dt_pre = lax.dynamic_slice_in_dim(summed_all[3], first_row, batch_dev, 0)
    window_x = jnp.concatenate([conv_x.astype(jnp.float32), x_pre[:, None, :]], axis=1)
    x_conv = jax.nn.silu(jnp.sum(window_x * conv_wx[None], axis=1))
    taps_prev = conv_bc.shape[1]
    bc_state = lax.dynamic_slice_in_dim(
        conv_bc.reshape(batch_dev, taps_prev, 2, G, N), my_group, 1, 3
    ).reshape(batch_dev, taps_prev, 2 * N)
    bc_taps = lax.dynamic_slice_in_dim(
        conv_wbc.reshape(taps_prev + 1, 2, G, N), my_group, 1, 2
    ).reshape(taps_prev + 1, 2 * N)
    window_bc = jnp.concatenate([bc_state.astype(jnp.float32), bc_pre[:, None, :]], axis=1)
    bc_conv = jax.nn.silu(jnp.sum(window_bc * bc_taps[None], axis=1)).reshape(batch_dev, 2, N)
    b_group = bc_conv[:, 0]
    c_group = bc_conv[:, 1]
    step_size = jax.nn.softplus(dt_pre + dt_bias[None])
    decay_rate = jnp.exp(-jnp.exp(a_log)[None] * step_size)
    x_heads = x_conv.reshape(batch_dev, heads_dev, P_SIZE)
    new_state = (
        decay_rate[:, :, None, None] * ssm_state
        + (step_size[:, :, None] * x_heads)[..., None] * b_group[:, None, None, :]
    )
    readout = jnp.einsum("bhpn,bn->bhp", new_state, c_group, precision=lax.Precision.HIGHEST)
    readout = readout + skip_gain[None, :, None] * x_heads
    gated = readout.reshape(batch_dev, heads_dev * P_SIZE) * jax.nn.silu(z_pre)
    group_total = jnp.sum(gated * gated, axis=-1)
    span_bits = group_span.bit_length() - 1
    for level in range(span_bits):
        partner = from_partner(group_total, "heads", level)
        group_total = group_total + partner
    mean_sq = group_total / (H * P_SIZE // G)
    inv_rms = lax.rsqrt(mean_sq + 1e-05)
    normed = (gated * inv_rms[:, None] * norm_gain[None]).astype(jnp.bfloat16)
    whole_rows = lax.all_gather(normed, "emb", axis=0, tiled=True)
    partial_value = jnp.dot(whole_rows, w_out, preferred_element_type=jnp.float32)
    mixed = lax.psum(partial_value, "heads").astype(jnp.bfloat16)
    return (mixed, new_state)


def solution(mesh):
    in_specs = (
        P(None, "emb"),
        P("emb", "heads"),
        P("emb", "heads"),
        P("emb", None),
        P("emb", "heads"),
        P("heads"),
        P("heads"),
        P("heads"),
        P("emb", None, "heads"),
        P("emb", None, None),
        P(None, "heads"),
        P(),
        P("emb", "heads", None, None),
        P("heads"),
        P("heads", "emb"),
    )
    out_specs = (P(None, "emb"), P("emb", "heads", None, None))
    return jax.shard_map(
        on_device, mesh=mesh, in_specs=in_specs, out_specs=out_specs, check_vma=False
    )
```

profile of v0, /device:TPU:0, one launch (start us, length us, event | category | flops | bytes accessed | tf_op | source)
XLA Modules:
  0.0 130.3 jit_solution(5878489030706171209)
XLA Ops:
  7.2 0.0 copy-start
  7.2 0.0 copy-start.3
  7.2 0.0 all-reduce.5.cloned.1.call-start
  7.2 0.0 copy-start.2
  7.2 5.4 %fusion.8 = f32[16,2048]{1,0:T(8,128)} fusion(bf16[16,2048]{1,0:T(8,128)(2,1)} %param.15, bf16[2048,2048]{1,0:T(8,128)(2,1)} %param.17), kind=kOutput, calls=%fused_computation.30 | convolution fusion | flops 134217728 | bytes 8585216 | tf_op jit(solution)/shard_map/dot_general | solution.py:44
  12.7 0.0 copy-done.3
  12.7 0.4 copy-done.2
  13.1 1.9 %fusion.9 = f32[16,2048]{1,0:T(8,128)} fusion(bf16[16,2048]{1,0:T(8,128)(2,1)S(1)} %copy-done.3, bf16[2048,2048]{1,0:T(8,128)(2,1)S(1)} %copy-done.2), kind=kOutput, calls=%fused_computation.31 | convolution fusion | flops 134217728 | bytes 8585216 | tf_op jit(solution)/shard_map/dot_general | solution.py:43
  15.0 0.0 all-reduce.5.cloned.1.call-update
  15.0 0.0 copy-start.4
  15.0 0.0 copy-start.5
  15.0 0.0 copy-start.11
  15.0 0.0 copy-start.6
  15.0 0.0 copy-start.10
  15.1 0.0 copy-start.7
  15.1 22.7 %copy.18 = bf16[2048,4096]{0,1:T(8,128)(2,1)} copy(bf16[2048,4096]{1,0:T(8,128)(2,1)} %param.18) | data formatting | bytes 33554432 | tf_op args[3]
  37.7 1.7 %constant_dynamic-slice_fusion = bf16[2048,2,1,256]{0,3,2,1:T(8,128)(2,1)S(1)} fusion(bf16[2048,2,8,256]{0,3,2,1:T(8,128)(2,1)} %bitcast.41, s32[]{:T(128)S(6)} %select_n.20), kind=kLoop, calls=%fused_computation.26 | loop fusion | bytes 4194308 | tf_op jit(solution)/shard_map/dynamic_slice | solution.py:40
  39.5 0.6 convolution_bitcast_fusion
  40.1 0.0 copy-done
  40.1 0.2 fusion.7
  40.3 0.0 copy-done.4
  40.3 0.1 reshape.54
  40.4 0.1 convert_reduce_fusion
  40.5 0.0 copy-done.5
  40.6 13.2 %all-reduce = (f32[16,512]{1,0:T(8,128)S(1)}, f32[16,32]{1,0:T(8,128)S(1)}) all-reduce(f32[16,512]{1,0:T(8,128)S(1)} %convolution_bitcast_fusion, f32[16,32]{1,0:T(8,128)S(1)} %fusion.7), channel_id=1, replica_groups=mesh['emb'=4,'heads'=8] {'emb'}, use_global_device_ids=true, to_apply=%region_3.4 | all-reduce | flops 8704 | bytes 69632 | tf_op jit(solution)/shard_map/psum | solution.py:47
  53.8 0.0 copy-done.11
  53.8 0.0 copy-done.6
  53.9 0.0 copy-done.10
  53.9 0.0 all-reduce.5.cloned.1.call-done
  53.9 0.9 dynamic-slice_bitcast_fusion
  54.8 0.0 copy-done.7
  54.9 0.1 reduce_sum.32
  55.0 0.1 broadcast_multiply_fusion
  55.0 4.7 %multiply_add_fusion = f32[4,32,64,256]{3,2,1,0:T(8,128)S(1)} fusion(f32[4,32,64,256]{3,2,1,0:T(8,128)} %param.27, f32[4,256]{1,0:T(4,128)S(1)} %get-tuple-element.11, f32[4,32,64]{2,1,0:T(8,128)S(1)} %broadcast_multiply_fusion, f32[4,32]{1,0:T(4,128)S(1)} %get-tuple-element.8), kind=kLoop, calls=%fused_computation | loop fusion | flops 6291456 | bytes 16814592 | tf_op jit(solution)/shard_map/add | solution.py:70
  59.8 0.0 copy-start.1
  59.8 0.0 copy-start.9
  59.8 0.0 copy-start.8
  59.8 3.4 %copy-done.1 = f32[4,32,64,256]{3,2,1,0:T(8,128)} copy-done((f32[4,32,64,256]{3,2,1,0:T(8,128)}, f32[4,32,64,256]{3,2,1,0:T(8,128)S(1)}, u32[]{:S(2)}) %copy-start.1) | copy-done | bytes 8388632
  63.2 9.8 %fusion.4 = f32[4,1,32,64]{3,1,2,0:T(1,128)S(1)} fusion(f32[4,32,64,256]{3,2,1,0:T(8,128)S(1)} %multiply_add_fusion, f32[4,256,1,1]{1,0,2,3:T(4,128)S(1)} %get-tuple-element.10), kind=kOutput, calls=%fused_computation.23 | convolution fusion | flops 25165824 | bytes 8425472 | tf_op jit(solution)/shard_map/bhpn,bn->bhp/dot_general | solution.py:73
  73.0 0.0 copy-done.9
  73.0 0.1 multiply_add_fusion.1
  73.1 0.1 reshape.58
  73.2 1.0 multiply_reduce_fusion
  74.2 0.0 copy-done.8
  74.2 0.1 fusion.3
  74.3 5.2 %all-gather = bf16[4,4,2048]{2,1,0:T(4,128)(2,1)S(1)} all-gather(bf16[1,4,2048]{2,1,0:T(4,128)(2,1)S(1)} %fusion.3), channel_id=1, replica_groups=mesh['emb'=4,'heads'=8] {'emb'}, dimensions={0}, use_global_device_ids=true | all-gather | bytes 81920 | tf_op jit(solution)/shard_map/all_gather | solution.py:84
  79.6 4.6 %fusion.10 = f32[16,2048]{1,0:T(8,128)S(1)} fusion(bf16[16,2048]{1,0:T(8,128)(2,1)S(1)} %reshape.61, bf16[2048,2048]{1,0:T(8,128)(2,1)} %param.29), kind=kOutput, calls=%fused_computation.32 | convolution fusion | flops 134217728 | bytes 8585216 | tf_op jit(solution)/shard_map/dot_general | solution.py:85
  84.1 39.3 %all-reduce.6 = bf16[16,2048]{1,0:T(8,128)(2,1)} all-reduce(f32[16,2048]{1,0:T(8,128)S(1)} %fusion.10), channel_id=1, replica_groups=mesh['emb'=4,'heads'=8] {'heads'}, use_global_device_ids=true, to_apply=%region_7.8 | all-reduce | flops 32768 | bytes 196608 | tf_op jit(solution)/shard_map/psum | solution.py:86
  (14 shorter events, 0.3 us)
Async XLA Ops:
  7.2 33.0 %copy-start = (bf16[2048,32]{0,1:T(8,128)(2,1)S(1)}, bf16[2048,32]{0,1:T(8,128)(2,1)}, u32[]{:S(2)}) copy-start(bf16[2048,32]{0,1:T(8,128)(2,1)} %param.19) | copy-start | bytes 393220
  7.2 5.5 %copy-start.3 = (bf16[16,2048]{1,0:T(8,128)(2,1)S(1)}, bf16[16,2048]{1,0:T(8,128)(2,1)}, u32[]{:S(2)}) copy-start(bf16[16,2048]{1,0:T(8,128)(2,1)} %param.15) | copy-start | bytes 196612
  7.2 46.7 %all-reduce.5.cloned.1.call-start = ((), (), s32[]{:S(2)}) async-start(), calls=%async_computation | async-start | bytes 524288 | tf_op jit(solution)/shard_map/psum | solution.py:47
  7.2 5.9 %copy-start.2 = (bf16[2048,2048]{1,0:T(8,128)(2,1)S(1)}, bf16[2048,2048]{1,0:T(8,128)(2,1)}, u32[]{:S(2)}) copy-start(bf16[2048,2048]{1,0:T(8,128)(2,1)} %param.16) | copy-start | bytes 25165828
  15.0 25.3 %copy-start.4 = (bf16[4,3,4096]{2,0,1:T(4,128)(2,1)S(1)}, bf16[4,3,4096]{2,0,1:T(4,128)(2,1)}, u32[]{:S(2)}) copy-start(bf16[4,3,4096]{2,0,1:T(4,128)(2,1)} %param.24) | copy-start | bytes 294916
  15.0 25.5 %copy-start.5 = (f32[4,4096]{1,0:T(4,128)S(1)}, f32[4,4096]{1,0:T(4,128)}, u32[]{:S(2)}) copy-start(f32[4,4096]{1,0:T(4,128)} %param.26) | copy-start | bytes 196612
  15.0 38.8 %copy-start.11 = (f32[32]{0:T(128)S(1)}, f32[32]{0:T(128)}, u32[]{:S(2)}) copy-start(f32[32]{0:T(128)} %param.21) | copy-start | bytes 388
  15.0 38.8 %copy-start.6 = (bf16[4,3,2048]{2,0,1:T(4,128)(2,1)S(1)}, bf16[4,3,2048]{2,0,1:T(4,128)(2,1)}, u32[]{:S(2)}) copy-start(bf16[4,3,2048]{2,0,1:T(4,128)(2,1)} %param.23) | copy-start | bytes 147460
  15.0 38.8 %copy-start.10 = (f32[32]{0:T(128)S(1)}, f32[32]{0:T(128)}, u32[]{:S(2)}) copy-start(f32[32]{0:T(128)} %param.20) | copy-start | bytes 388
  15.1 39.7 %copy-start.7 = (f32[4,2048]{1,0:T(4,128)S(1)}, f32[4,2048]{1,0:T(4,128)}, u32[]{:S(2)}) copy-start(f32[4,2048]{1,0:T(4,128)} %param.25) | copy-start | bytes 98308
  59.8 3.4 %copy-start.1 = (f32[4,32,64,256]{3,2,1,0:T(8,128)}, f32[4,32,64,256]{3,2,1,0:T(8,128)S(1)}, u32[]{:S(2)}) copy-start(f32[4,32,64,256]{3,2,1,0:T(8,128)S(1)} %multiply_add_fusion) | copy-start | bytes 25165828
  59.8 13.2 %copy-start.9 = (f32[32]{0:T(128)S(1)}, f32[32]{0:T(128)}, u32[]{:S(2)}) copy-start(f32[32]{0:T(128)} %param.22) | copy-start | bytes 388
  59.8 14.4 %copy-start.8 = (f32[2048]{0:T(1024)S(1)}, f32[2048]{0:T(1024)}, u32[]{:S(2)}) copy-start(f32[2048]{0:T(1024)} %param.28) | copy-start | bytes 24580
Sparse Core Ops, SparseCore 0:
  15.1 35.0 all-reduce.4
where the time goes:
time: 131 us; the launch traced here: 130 us
  blocking collectives  57.7 us (44%)
  local copies, waits for them, and re-layouts  29.5 us (23%)
  matrix products  22.5 us (17%)
  between operations  14.3 us (11%)
  other arithmetic  6.23 us (5%)
    psum x1, blocking collectives, on_device(): mixed = lax.psum(partial_value, 'heads').astype(jnp.bfloat16)  39.3 us
    unnamed x28, local copies, waits for them, and re-layouts  26.6 us
    psum x1, blocking collectives, on_device(): summed_all = lax.psum((z_part, x_part, bc_part, dt_part), 'emb')  13.2 us
    dot_general x1, matrix products, on_device(): jnp.einsum('bhpn,bn->bhp', new_state, c_group, precision=lax.Precision.HI...  9.83 us
    dot_general x1, matrix products, on_device(): x_part = jnp.dot(hidden_in, w_x, preferred_element_type=jnp.float32)  5.43 us
    all_gather x1, blocking collectives, on_device(): whole_rows = lax.all_gather(normed, 'emb', axis=0, tiled=True)  5.23 us
    add x1, other arithmetic, on_device(): decay_rate[:, :, None, None] * ssm_state  4.75 us
    dot_general x1, matrix products, on_device(): jnp.dot(whole_rows, w_out, preferred_element_type=jnp.float32)  4.58 us
  transfers between devices with their start and end apart: 1, of which 0 were waited for; matrix products, arithmetic and copies ran while one was open for 20% of the time, Pallas kernels for 0%

commit v1 on v0

v1 whole, which is shorter than its diff:
```python
import functools

import jax
import jax.numpy as jnp
from jax import lax
from jax.experimental import pallas as pl
from jax.experimental.pallas import tpu as pltpu
from jax.sharding import PartitionSpec as P

H = 256
P_SIZE = 64
N = 256
G = 8
LANES = 128
DEPTH = 6
MESH = pl.DeviceIdType.MESH
F32 = jnp.float32
BF16 = jnp.bfloat16


def silu(v):
    return v / (1.0 + jnp.exp(-v))


def softplus(v):
    return jnp.maximum(v, 0.0) + jnp.log1p(jnp.exp(-jnp.abs(v)))


def split3(v):
    high = v.astype(BF16)
    rest = v - high.astype(F32)
    mid = rest.astype(BF16)
    low = (rest - mid.astype(F32)).astype(BF16)
    return high, mid, low


def kernel(
    dims,
    hidden_ref,
    dtb_ref,
    alog_ref,
    skip_ref,
    convx_ref,
    convwx_ref,
    gain_ref,
    wz_hbm,
    wx_hbm,
    wbc_hbm,
    wdt_hbm,
    convbc_hbm,
    convwbc_hbm,
    state_hbm,
    wout_hbm,
    out_ref,
    st_ref,
    wz_v,
    wx_v,
    wbc_v,
    wdt_v,
    convbc_v,
    convwbc_v,
    wout_v,
    xsend,
    xrecv,
    zsend,
    zrecv,
    cols_v,
    read_v,
    xc_v,
    ag_v,
    rs_send,
    rs_recv,
    fin_send,
    fin_v,
    sq_send,
    sq_recv,
    dma_sem,
    x_ss,
    x_rs,
    z_ss,
    z_rs,
    a_ss,
    a_rs,
    r_ss,
    r_rs,
    f_ss,
    f_rs,
    q_ss,
    q_rs,
):
    n_emb, n_heads, batch, bd, di, hd, cols, chunk, ochunk, fused, span = dims
    e = lax.axis_index("emb")
    h = lax.axis_index("heads")
    group = h // span

    def emb_peer(o):
        return lax.rem(e + o, n_emb)

    def head_peer(o):
        return lax.rem(h + o, n_heads)

    copies = {}
    order = []

    def stream(name, src, dst):
        copies[name] = pltpu.make_async_copy(src, dst, dma_sem.at[len(order)])
        order.append(name)

    for half in range(2):
        off = pl.multiple_of(half * G * N + group * N, N)
        stream(("bc", half), wbc_hbm.at[:, pl.ds(off, N)], wbc_v.at[half])
    stream(("dt", 0), wdt_hbm, wdt_v)
    for half in range(2):
        off = pl.multiple_of(half * G * N + group * N, N)
        stream(("cb", half), convbc_hbm.at[:, :, pl.ds(off, N)], convbc_v.at[half])
        stream(("cw", half), convwbc_hbm.at[:, pl.ds(off, N)], convwbc_v.at[half])
    n_chunk = di // chunk
    for c in range(n_chunk):
        stream(("x", c), wx_hbm.at[:, pl.ds(c * chunk, chunk)], wx_v.at[c])
    for c in range(n_chunk):
        stream(("z", c), wz_hbm.at[:, pl.ds(c * chunk, chunk)], wz_v.at[c])
    for b in range(bd):
        stream(("s", b), state_hbm.at[b], st_ref.at[b])
    n_out = cols // ochunk
    for i in range(n_out):
        at = lax.rem(h + i + 1, n_heads) if fused else i
        off = pl.multiple_of(at * ochunk, ochunk)
        stream(("o", i), wout_hbm.at[:, pl.ds(off, ochunk)], wout_v.at[i])
    started = [0]

    def advance():
        if started[0] < len(order):
            copies[order[started[0]]].start()
            started[0] += 1

    def ready(name):
        copies[name].wait()
        advance()

    for _ in range(DEPTH + 6):
        advance()

    barrier = pltpu.get_barrier_semaphore()
    for o in range(1, n_emb):
        pl.semaphore_signal(barrier, inc=1, device_id={"emb": emb_peer(o)}, device_id_type=MESH)
    n_greet = n_emb - 1
    if fused:
        for o in range(1, n_heads):
            pl.semaphore_signal(
                barrier, inc=1, device_id={"heads": head_peer(o)}, device_id_type=MESH
            )
        n_greet += n_heads - 1
    elif span > 1:
        for o in range(1, span):
            pl.semaphore_signal(
                barrier,
                inc=1,
                device_id={"heads": group * span + lax.rem(h % span + o, span)},
                device_id_type=MESH,
            )
        n_greet += span - 1

    hidden = hidden_ref[...]

    def project(weights, send, at, width):
        part = jnp.dot(hidden, weights, preferred_element_type=F32)
        for peer in range(n_emb):
            send[peer, :, at : at + width] = part[peer * bd : (peer + 1) * bd]

    heads_at = lax.broadcasted_iota(jnp.int32, (hd, di), 0)
    chans_at = lax.broadcasted_iota(jnp.int32, (hd, di), 1)
    lower = heads_at * P_SIZE
    expand = jnp.where((chans_at >= lower) & (chans_at < lower + P_SIZE), 1.0, 0.0).astype(BF16)

    def conv_prev(values, taps, k):
        rows = [
            jnp.sum(values[b].astype(F32) * taps[0:k], axis=0, keepdims=True) for b in range(bd)
        ]
        return jnp.concatenate(rows, axis=0)

    k_prev = convx_ref.shape[1]
    x_base = conv_prev(convx_ref, convwx_ref[...], k_prev)

    for half in range(2):
        ready(("bc", half))
        project(wbc_v[half], xsend, di + half * N, N)
    ready(("dt", 0))
    xsend[:, :, di + 2 * N :] = jnp.zeros((n_emb, bd, LANES), F32)
    project(wdt_v[...], xsend, di + 2 * N, hd)
    bc_base = []
    for half in range(2):
        ready(("cb", half))
        ready(("cw", half))
        bc_base.append(conv_prev(convbc_v.at[half], convwbc_v[half], k_prev))
    for c in range(n_chunk):
        ready(("x", c))
        project(wx_v[c], xsend, c * chunk, chunk)

    pl.semaphore_wait(barrier, n_greet)

    def send_emb(src, dst, ss, rs):
        made = []
        for o in range(n_emb - 1, 0, -1):
            peer = emb_peer(o)
            copy = pltpu.make_async_remote_copy(
                src_ref=src.at[peer],
                dst_ref=dst.at[o - 1],
                send_sem=ss.at[o - 1],
                recv_sem=rs.at[o - 1],
                device_id={"emb": peer},
                device_id_type=MESH,
            )
            copy.start()
            made.append(copy)
        return made

    x_copies = send_emb(xsend, xrecv, x_ss, x_rs)
    for c in range(n_chunk):
        ready(("z", c))
        project(wz_v[c], zsend, c * chunk, chunk)
    z_copies = send_emb(zsend, zrecv, z_ss, z_rs)

    for copy in x_copies:
        copy.wait_recv()
    xall = xsend[e]
    for o in range(n_emb - 1):
        xall = xall + xrecv[o]
    x_conv = silu(x_base + xall[:, 0:di] * convwx_ref[k_prev : k_prev + 1, :])
    bc = []
    for half in range(2):
        pre = xall[:, di + half * N : di + (half + 1) * N]
        bc.append(silu(bc_base[half] + pre * convwbc_v[half, k_prev : k_prev + 1, :]))
    b_group, c_group = bc
    dt_pre = xall[:, di + 2 * N : di + 2 * N + hd]
    step = softplus(dt_pre + dtb_ref[...])
    decay = jnp.exp(-jnp.exp(alog_ref[...]) * step)
    skip = jnp.broadcast_to(skip_ref[...], (bd, hd))
    by_head = jnp.concatenate([step, decay, skip], axis=0)
    by_chan = sum(jnp.dot(part, expand, preferred_element_type=F32) for part in split3(by_head))
    step_c = by_chan[0:bd]
    decay_c = by_chan[bd : 2 * bd]
    skip_c = by_chan[2 * bd : 3 * bd]
    rows = jnp.concatenate([step_c * x_conv, decay_c], axis=0)
    cols_v[...] = jnp.transpose(rows)
    xc_v[...] = skip_c * x_conv
    c_high, c_low, _ = split3(c_group)
    c_both = jnp.concatenate([c_high.astype(F32), c_low.astype(F32)], axis=0).astype(BF16)

    rows_at = 256 if di % 256 == 0 else di
    for b in range(bd):
        ready(("s", b))
        b_row = b_group[b : b + 1, :]

        def update(i, carry, b=b, b_row=b_row):
            at = pl.ds(pl.multiple_of(i * rows_at, rows_at), rows_at)
            xcol = cols_v[at, b : b + 1]
            dcol = cols_v[at, bd + b : bd + b + 1]
            new = dcol * st_ref[b, at, :] + xcol * b_row
            st_ref[b, at, :] = new
            got = lax.dot_general(
                c_both, new.astype(BF16), (((1,), (1,)), ((), ())), preferred_element_type=F32
            )
            read_v[b : b + 1, at] = got[b : b + 1, :] + got[bd + b : bd + b + 1, :]
            return carry

        lax.fori_loop(0, di // rows_at, update, 0)

    for copy in z_copies:
        copy.wait_recv()
    zall = zsend[e]
    for o in range(n_emb - 1):
        zall = zall + zrecv[o]
    gated = (read_v[...] + xc_v[...]) * silu(zall)
    total = jnp.sum(gated * gated, axis=1, keepdims=True)
    q_copies = []
    if span > 1:
        sq_send[...] = jnp.broadcast_to(total, (bd, LANES))
        for o in range(1, span):
            copy = pltpu.make_async_remote_copy(
                src_ref=sq_send,
                dst_ref=sq_recv.at[o - 1],
                send_sem=q_ss.at[o - 1],
                recv_sem=q_rs.at[o - 1],
                device_id={"heads": group * span + lax.rem(h % span + o, span)},
                device_id_type=MESH,
            )
            copy.start()
            q_copies.append(copy)
        for o, copy in enumerate(q_copies):
            copy.wait_recv()
            total = total + sq_recv[o][:, 0:1]
    inv_rms = lax.rsqrt(total / (H * P_SIZE // G) + 1e-05)
    normed = (gated * inv_rms * gain_ref[...]).astype(BF16)
    ag_v[e] = normed
    a_copies = []
    for o in range(n_emb - 1, 0, -1):
        copy = pltpu.make_async_remote_copy(
            src_ref=ag_v.at[e],
            dst_ref=ag_v.at[e],
            send_sem=a_ss.at[o - 1],
            recv_sem=a_rs.at[o - 1],
            device_id={"emb": emb_peer(o)},
            device_id_type=MESH,
        )
        copy.start()
        a_copies.append(copy)
    for copy in a_copies:
        copy.wait_recv()
    whole = jnp.concatenate([ag_v[i].astype(F32) for i in range(n_emb)], axis=0).astype(BF16)

    last = []
    own = None
    for i in range(n_out):
        ready(("o", i))
        part = jnp.dot(whole, wout_v[i], preferred_element_type=F32)
        if not fused:
            out_ref[:, i * ochunk : (i + 1) * ochunk] = part
        elif i < n_out - 1:
            rs_send[i] = part.astype(BF16)
            copy = pltpu.make_async_remote_copy(
                src_ref=rs_send.at[i],
                dst_ref=rs_recv.at[i],
                send_sem=r_ss.at[i],
                recv_sem=r_rs.at[i],
                device_id={"heads": head_peer(i + 1)},
                device_id_type=MESH,
            )
            copy.start()
            last.append(copy)
        else:
            own = part
    f_copies = []
    if fused:
        for i, copy in enumerate(last):
            copy.wait_recv()
            own = own + rs_recv[i].astype(F32)
        fin_send[...] = own.astype(BF16)
        for o in range(1, n_heads):
            copy = pltpu.make_async_remote_copy(
                src_ref=fin_send,
                dst_ref=fin_v.at[h],
                send_sem=f_ss.at[o - 1],
                recv_sem=f_rs.at[o - 1],
                device_id={"heads": head_peer(o)},
                device_id_type=MESH,
            )
            copy.start()
            f_copies.append(copy)
        fin_v[h] = fin_send[...]
        for copy in f_copies:
            copy.wait_recv()
        for i in range(n_heads):
            out_ref[:, i * ochunk : (i + 1) * ochunk] = fin_v[i]
    for copy in x_copies + z_copies + q_copies + a_copies + last + f_copies:
        copy.wait_send()


def on_device(
    hidden_in,
    w_z,
    w_x,
    w_bc,
    w_dt,
    dt_bias,
    a_log,
    skip_gain,
    conv_x,
    conv_bc,
    conv_wx,
    conv_wbc,
    ssm_state,
    norm_gain,
    w_out,
):
    n_emb = lax.axis_size("emb")
    n_heads = lax.axis_size("heads")
    span = n_heads // G
    batch, depth = hidden_in.shape
    bd = conv_x.shape[0]
    k_prev = conv_x.shape[1]
    di = w_x.shape[1]
    hd = w_dt.shape[1]
    cols = w_out.shape[1]
    fused = cols % (n_heads * LANES) == 0
    chunk = min(512, di)
    ochunk = cols // n_heads if fused else min(256, cols)
    dims = (n_emb, n_heads, batch, bd, di, hd, cols, chunk, ochunk, fused, span)
    n_chunk = di // chunk
    n_out = cols // ochunk
    x_cols = di + 2 * N + LANES
    n_streams = 7 + 2 * n_chunk + bd + n_out
    vm = pl.BlockSpec(memory_space=pltpu.VMEM)
    hbm = pl.BlockSpec(memory_space=pl.ANY)
    dma = pltpu.SemaphoreType.DMA
    rs_n = max(n_heads - 1, 1) if fused else 1
    rs_shape = (batch, ochunk) if fused else (batch, LANES)
    fin_n = n_heads if fused else 1
    e_n = max(n_emb - 1, 1)
    q_n = max(span - 1, 1)
    out, new_state = pl.pallas_call(
        functools.partial(kernel, dims),
        out_shape=(
            jax.ShapeDtypeStruct((batch, cols), BF16 if fused else F32),
            pltpu.VMEM((bd, di, N), F32),
        ),
        in_specs=[vm] * 7 + [hbm] * 8,
        out_specs=(vm, vm),
        scratch_shapes=[
            pltpu.VMEM((n_chunk, depth, chunk), BF16),
            pltpu.VMEM((n_chunk, depth, chunk), BF16),
            pltpu.VMEM((2, depth, N), BF16),
            pltpu.VMEM((depth, hd), BF16),
            pltpu.VMEM((2, bd, k_prev, N), BF16),
            pltpu.VMEM((2, k_prev + 1, N), F32),
            pltpu.VMEM((n_out, w_out.shape[0], ochunk), BF16),
            pltpu.VMEM((n_emb, bd, x_cols), F32),
            pltpu.VMEM((e_n, bd, x_cols), F32),
            pltpu.VMEM((n_emb, bd, di), F32),
            pltpu.VMEM((e_n, bd, di), F32),
            pltpu.VMEM((di, 2 * bd), F32),
            pltpu.VMEM((bd, di), F32),
            pltpu.VMEM((bd, di), F32),
            pltpu.VMEM((n_emb, bd, di), BF16),
            pltpu.VMEM((rs_n,) + rs_shape, BF16),
            pltpu.VMEM((rs_n,) + rs_shape, BF16),
            pltpu.VMEM(rs_shape, BF16),
            pltpu.VMEM((fin_n,) + rs_shape, BF16),
            pltpu.VMEM((bd, LANES), F32),
            pltpu.VMEM((q_n, bd, LANES), F32),
            dma((n_streams,)),
            dma((e_n,)),
            dma((e_n,)),
            dma((e_n,)),
            dma((e_n,)),
            dma((e_n,)),
            dma((e_n,)),
            dma((rs_n,)),
            dma((rs_n,)),
            dma((rs_n,)),
            dma((rs_n,)),
            dma((q_n,)),
            dma((q_n,)),
        ],
        compiler_params=pltpu.CompilerParams(
            collective_id=0, has_side_effects=True, vmem_limit_bytes=44 * 1024 * 1024
        ),
    )(
        hidden_in,
        dt_bias.reshape(1, hd),
        a_log.reshape(1, hd),
        skip_gain.reshape(1, hd),
        conv_x,
        conv_wx,
        norm_gain.reshape(1, di),
        w_z,
        w_x,
        w_bc,
        w_dt,
        conv_bc,
        conv_wbc,
        ssm_state.reshape(bd, di, N),
        w_out,
    )
    mixed = out if fused else lax.psum(out, "heads").astype(BF16)
    return (mixed, new_state.reshape(bd, hd, P_SIZE, N))


def solution(mesh):
    in_specs = (
        P(None, "emb"),
        P("emb", "heads"),
        P("emb", "heads"),
        P("emb", None),
        P("emb", "heads"),
        P("heads"),
        P("heads"),
        P("heads"),
        P("emb", None, "heads"),
        P("emb", None, None),
        P(None, "heads"),
        P(),
        P("emb", "heads", None, None),
        P("heads"),
        P("heads", "emb"),
    )
    out_specs = (P(None, "emb"), P("emb", "heads", None, None))
    return jax.shard_map(
        on_device, mesh=mesh, in_specs=in_specs, out_specs=out_specs, check_vma=False
    )
```

time: 131 us -> 47.7 us (0.36)
  blocking collectives: 57.7 us -> 0 us
  Pallas kernels: 0 us -> 34.5 us
  matrix products: 22.5 us -> 0 us
  local copies, waits for them, and re-layouts: 29.5 us -> 12.1 us
  between operations: 14.3 us -> 0.66 us
  other arithmetic: 6.23 us -> 0 us
    psum x2 -> x0, blocking collectives: 52.4 us -> none  [the longest x1 39.3 us: on_device(): mixed = lax.psum(partial_value, 'heads').astype(jnp.bfloat16)]
    pallas_call x0 -> x1, Pallas kernels: none -> 34.5 us  [on_device(): pl.pallas_call(functools.partial(kernel, dims), out_shape=(jax.ShapeDtype...]
    dot_general x6 -> x0, matrix products: 22.5 us -> none  [the longest x1 9.83 us: on_device(): jnp.einsum('bhpn,bn->bhp', new_state, c_group, precision=lax.Precision.HI...]
    unnamed x28 -> x19, local copies, waits for them, and re-layouts: 26.6 us -> 12.1 us
    all_gather x1 -> x0, blocking collectives: 5.23 us -> none  [on_device(): whole_rows = lax.all_gather(normed, 'emb', axis=0, tiled=True)]
    add x2 -> x0, other arithmetic: 4.84 us -> none  [the longest x1 4.75 us: on_device(): decay_rate[:, :, None, None] * ssm_state]
    dynamic_slice x2 -> x0, local copies, waits for them, and re-layouts: 1.78 us -> none  [the longest x1 1.74 us: on_device(): lax.dynamic_slice_in_dim(w_bc.reshape(emb_rows, 2, G, N), my_group, 1, 2)]
  transfers between devices with their start and end apart: 1 -> 0, of which waited for: 0 -> 0; matrix products, arithmetic and copies ran while one was open for 20% -> 0% of each run, Pallas kernels for 0% -> 0%
where the time goes in v1:
time: 47.7 us; the launch traced here: 47.2 us
  Pallas kernels  34.5 us (72%)
  local copies, waits for them, and re-layouts  12.1 us (25%)
  between operations  0.66 us (1%)
    pallas_call x1, Pallas kernels, on_device(): pl.pallas_call(functools.partial(kernel, dims), out_shape=(jax.ShapeDtype...  34.5 us
    unnamed x19, local copies, waits for them, and re-layouts  12.1 us

profile of v1, /device:TPU:0, one launch (start us, length us, event | category | flops | bytes accessed | tf_op | source)
XLA Modules:
  0.0 47.2 jit_solution(24945900393827207)
XLA Ops:
  0.6 0.8 %copy.17.convx_ref = bf16[4,3,2048]{2,1,0:T(4,128)(2,1)S(1)} copy(bf16[4,3,2048]{2,0,1:T(4,128)(2,1)} %param.23) | data formatting | bytes 98304 | tf_op args[8]
  1.5 1.0 %copy.19.convbc_hbm = bf16[4,3,4096]{2,1,0:T(4,128)(2,1)S(1)} copy(bf16[4,3,4096]{2,0,1:T(4,128)(2,1)} %param.24) | data formatting | bytes 196608 | tf_op args[9]
  2.5 1.2 %copy.18.wdt_hbm = bf16[2048,32]{1,0:T(8,128)(2,1)S(1)} copy(bf16[2048,32]{0,1:T(8,128)(2,1)} %param.19) | data formatting | bytes 262144 | tf_op args[4]
  3.6 0.0 copy-start
  3.7 0.8 %copy-done = bf16[16,2048]{1,0:T(8,128)(2,1)S(1)} copy-done((bf16[16,2048]{1,0:T(8,128)(2,1)S(1)}, bf16[16,2048]{1,0:T(8,128)(2,1)}, u32[]{:S(2)}) %copy-start) | copy-done | bytes 65560
  4.5 0.0 copy-start.1
  4.5 0.8 %copy-done.1 = f32[4,4096]{1,0:T(4,128)S(1)} copy-done((f32[4,4096]{1,0:T(4,128)S(1)}, f32[4,4096]{1,0:T(4,128)}, u32[]{:S(2)}) %copy-start.1) | copy-done | bytes 65560
  5.3 0.0 copy-start.2
  5.3 0.8 %copy-done.2 = f32[4,2048]{1,0:T(4,128)S(1)} copy-done((f32[4,2048]{1,0:T(4,128)S(1)}, f32[4,2048]{1,0:T(4,128)}, u32[]{:S(2)}) %copy-start.2) | copy-done | bytes 32792
  6.1 0.0 copy-start.3
  6.1 0.7 %copy-done.3 = f32[2048]{0:T(1024)S(1)} copy-done((f32[2048]{0:T(1024)S(1)}, f32[2048]{0:T(1024)}, u32[]{:S(2)}) %copy-start.3) | copy-done | bytes 8216
  6.8 0.0 copy-start.4
  6.8 0.7 %copy-done.4 = f32[32]{0:T(128)S(1)} copy-done((f32[32]{0:T(128)S(1)}, f32[32]{0:T(128)}, u32[]{:S(2)}) %copy-start.4) | copy-done | bytes 152
  7.4 0.0 copy-start.5
  7.4 0.7 %copy-done.5 = f32[32]{0:T(128)S(1)} copy-done((f32[32]{0:T(128)S(1)}, f32[32]{0:T(128)}, u32[]{:S(2)}) %copy-start.5) | copy-done | bytes 152
  8.1 0.0 copy-start.6
  8.1 0.7 %copy-done.6 = f32[32]{0:T(128)S(1)} copy-done((f32[32]{0:T(128)S(1)}, f32[32]{0:T(128)}, u32[]{:S(2)}) %copy-start.6) | copy-done | bytes 152
  8.8 34.5 %shard_map.158 = (bf16[16,2048]{1,0:T(8,128)(2,1)S(1)}, f32[4,2048,256]{2,1,0:T(8,128)S(1)}) custom-call(bf16[16,2048]{1,0:T(8,128)(2,1)S(1)} %copy-done, f32[1,32]{1,0:T(1,128)S(1)} %bitcast.8, f32[1,32]{1,0:T(1,128)S(1)} %bitcast.9, f32[1,32]{1,0:T(1,128)S(1)} %bitcast.10, bf16[4,3,2048]{2,1,0:T(4,128)(2,1)S(1)} %copy.17.convx_ref, ...), custom_call_target="tpu_custom_call" | custom-call | tf_op jit(solution)/shard_map/pallas_call | solution.py:400
  43.2 3.4 %copy.22 = f32[4,32,64,256]{3,2,1,0:T(8,128)} copy(f32[4,32,64,256]{3,2,1,0:T(8,128)S(1)} %bitcast.6) | data formatting | bytes 16777216
  46.6 0.6 %copy.23 = bf16[16,2048]{1,0:T(8,128)(2,1)} copy(bf16[16,2048]{1,0:T(8,128)(2,1)S(1)} %get-tuple-element.10) | data formatting | bytes 131072
Async XLA Ops:
  3.6 0.8 %copy-start = (bf16[16,2048]{1,0:T(8,128)(2,1)S(1)}, bf16[16,2048]{1,0:T(8,128)(2,1)}, u32[]{:S(2)}) copy-start(bf16[16,2048]{1,0:T(8,128)(2,1)} %hidden_ref.1) | copy-start | bytes 196612
  4.5 0.8 %copy-start.1 = (f32[4,4096]{1,0:T(4,128)S(1)}, f32[4,4096]{1,0:T(4,128)}, u32[]{:S(2)}) copy-start(f32[4,4096]{1,0:T(4,128)} %convwbc_hbm.1) | copy-start | bytes 196612
  5.3 0.8 %copy-start.2 = (f32[4,2048]{1,0:T(4,128)S(1)}, f32[4,2048]{1,0:T(4,128)}, u32[]{:S(2)}) copy-start(f32[4,2048]{1,0:T(4,128)} %convwx_ref.1) | copy-start | bytes 98308
  6.1 0.7 %copy-start.3 = (f32[2048]{0:T(1024)S(1)}, f32[2048]{0:T(1024)}, u32[]{:S(2)}) copy-start(f32[2048]{0:T(1024)} %param.28) | copy-start | bytes 24580
  6.8 0.7 %copy-start.4 = (f32[32]{0:T(128)S(1)}, f32[32]{0:T(128)}, u32[]{:S(2)}) copy-start(f32[32]{0:T(128)} %param.20) | copy-start | bytes 388
  7.4 0.7 %copy-start.5 = (f32[32]{0:T(128)S(1)}, f32[32]{0:T(128)}, u32[]{:S(2)}) copy-start(f32[32]{0:T(128)} %param.21) | copy-start | bytes 388
  8.1 0.7 %copy-start.6 = (f32[32]{0:T(128)S(1)}, f32[32]{0:T(128)}, u32[]{:S(2)}) copy-start(f32[32]{0:T(128)} %param.22) | copy-start | bytes 388

commit v2 on v1

--- a/solution.py
+++ b/solution.py
@@ -36,13 +36,13 @@
 
 def kernel(
     dims,
-    hidden_ref,
-    dtb_ref,
-    alog_ref,
-    skip_ref,
-    convx_ref,
-    convwx_ref,
-    gain_ref,
+    hidden_hbm,
+    dtb_hbm,
+    alog_hbm,
+    skip_hbm,
+    convx_hbm,
+    convwx_hbm,
+    gain_hbm,
     wz_hbm,
     wx_hbm,
     wbc_hbm,
@@ -53,6 +53,13 @@
     wout_hbm,
     out_ref,
     st_ref,
+    hidden_ref,
+    dtb_ref,
+    alog_ref,
+    skip_ref,
+    convx_v,
+    convwx_ref,
+    gain_ref,
     wz_v,
     wx_v,
     wbc_v,
@@ -106,6 +113,7 @@
         copies[name] = pltpu.make_async_copy(src, dst, dma_sem.at[len(order)])
         order.append(name)
 
+    stream("hidden", hidden_hbm, hidden_ref)
     for half in range(2):
         off = pl.multiple_of(half * G * N + group * N, N)
         stream(("bc", half), wbc_hbm.at[:, pl.ds(off, N)], wbc_v.at[half])
@@ -114,6 +122,12 @@
         off = pl.multiple_of(half * G * N + group * N, N)
         stream(("cb", half), convbc_hbm.at[:, :, pl.ds(off, N)], convbc_v.at[half])
         stream(("cw", half), convwbc_hbm.at[:, pl.ds(off, N)], convwbc_v.at[half])
+    stream("dtb", dtb_hbm, dtb_ref)
+    stream("alog", alog_hbm, alog_ref)
+    stream("skip", skip_hbm, skip_ref)
+    stream("convx", convx_hbm, convx_v)
+    stream("convwx", convwx_hbm, convwx_ref)
+    stream("gain", gain_hbm, gain_ref)
     n_chunk = di // chunk
     for c in range(n_chunk):
         stream(("x", c), wx_hbm.at[:, pl.ds(c * chunk, chunk)], wx_v.at[c])
@@ -137,7 +151,7 @@
         copies[name].wait()
         advance()
 
-    for _ in range(DEPTH + 6):
+    for _ in range(DEPTH + 12):
         advance()
 
     barrier = pltpu.get_barrier_semaphore()
@@ -160,6 +174,7 @@
             )
         n_greet += span - 1
 
+    ready("hidden")
     hidden = hidden_ref[...]
 
     def project(weights, send, at, width):
@@ -172,26 +187,29 @@
     lower = heads_at * P_SIZE
     expand = jnp.where((chans_at >= lower) & (chans_at < lower + P_SIZE), 1.0, 0.0).astype(BF16)
 
-    def conv_prev(values, taps, k):
-        rows = [
-            jnp.sum(values[b].astype(F32) * taps[0:k], axis=0, keepdims=True) for b in range(bd)
-        ]
-        return jnp.concatenate(rows, axis=0)
-
-    k_prev = convx_ref.shape[1]
-    x_base = conv_prev(convx_ref, convwx_ref[...], k_prev)
+    k_prev = convx_v.shape[0]
+
+    def conv_prev(values, taps):
+        return sum(values[k].astype(F32) * taps[k : k + 1, :] for k in range(k_prev))
 
     for half in range(2):
         ready(("bc", half))
         project(wbc_v[half], xsend, di + half * N, N)
     ready(("dt", 0))
     xsend[:, :, di + 2 * N :] = jnp.zeros((n_emb, bd, LANES), F32)
-    project(wdt_v[...], xsend, di + 2 * N, hd)
+    part = lax.dot_general(
+        hidden, wdt_v[...], (((1,), (1,)), ((), ())), preferred_element_type=F32
+    )
+    for peer in range(n_emb):
+        xsend[peer, :, di + 2 * N : di + 2 * N + hd] = part[peer * bd : (peer + 1) * bd]
     bc_base = []
     for half in range(2):
         ready(("cb", half))
         ready(("cw", half))
-        bc_base.append(conv_prev(convbc_v.at[half], convwbc_v[half], k_prev))
+        bc_base.append(conv_prev(convbc_v.at[half], convwbc_v[half]))
+    for name in ("dtb", "alog", "skip", "convx", "convwx", "gain"):
+        ready(name)
+    x_base = conv_prev(convx_v, convwx_ref[...])
     for c in range(n_chunk):
         ready(("x", c))
         project(wx_v[c], xsend, c * chunk, chunk)
@@ -353,6 +371,10 @@
             out_ref[:, i * ochunk : (i + 1) * ochunk] = fin_v[i]
     for copy in x_copies + z_copies + q_copies + a_copies + last + f_copies:
         copy.wait_send()
+
+
+def in_hbm(*arrays):
+    return [pltpu.with_memory_space_constraint(array, pltpu.HBM) for array in arrays]
 
 
 def on_device(
@@ -388,9 +410,9 @@
     n_chunk = di // chunk
     n_out = cols // ochunk
     x_cols = di + 2 * N + LANES
-    n_streams = 7 + 2 * n_chunk + bd + n_out
+    n_streams = 14 + 2 * n_chunk + bd + n_out
     vm = pl.BlockSpec(memory_space=pltpu.VMEM)
-    hbm = pl.BlockSpec(memory_space=pl.ANY)
+    hbm = pl.BlockSpec(memory_space=pltpu.HBM)
     dma = pltpu.SemaphoreType.DMA
     rs_n = max(n_heads - 1, 1) if fused else 1
     rs_shape = (batch, ochunk) if fused else (batch, LANES)
@@ -403,14 +425,21 @@
             jax.ShapeDtypeStruct((batch, cols), BF16 if fused else F32),
             pltpu.VMEM((bd, di, N), F32),
         ),
-        in_specs=[vm] * 7 + [hbm] * 8,
+        in_specs=[hbm] * 15,
         out_specs=(vm, vm),
         scratch_shapes=[
+            pltpu.VMEM((batch, depth), BF16),
+            pltpu.VMEM((1, hd), F32),
+            pltpu.VMEM((1, hd), F32),
+            pltpu.VMEM((1, hd), F32),
+            pltpu.VMEM((k_prev, bd, di), BF16),
+            pltpu.VMEM((k_prev + 1, di), F32),
+            pltpu.VMEM((1, di), F32),
             pltpu.VMEM((n_chunk, depth, chunk), BF16),
             pltpu.VMEM((n_chunk, depth, chunk), BF16),
             pltpu.VMEM((2, depth, N), BF16),
-            pltpu.VMEM((depth, hd), BF16),
-            pltpu.VMEM((2, bd, k_prev, N), BF16),
+            pltpu.VMEM((hd, depth), BF16),
+            pltpu.VMEM((2, k_prev, bd, N), BF16),
             pltpu.VMEM((2, k_prev + 1, N), F32),
             pltpu.VMEM((n_out, w_out.shape[0], ochunk), BF16),
             pltpu.VMEM((n_emb, bd, x_cols), F32),
@@ -445,21 +474,23 @@
             collective_id=0, has_side_effects=True, vmem_limit_bytes=44 * 1024 * 1024
         ),
     )(
+        *in_hbm(
         hidden_in,
         dt_bias.reshape(1, hd),
         a_log.reshape(1, hd),
         skip_gain.reshape(1, hd),
-        conv_x,
+        jnp.transpose(conv_x, (1, 0, 2)),
         conv_wx,
         norm_gain.reshape(1, di),
         w_z,
         w_x,
         w_bc,
-        w_dt,
-        conv_bc,
+        w_dt.T,
+        jnp.transpose(conv_bc, (1, 0, 2)),
         conv_wbc,
         ssm_state.reshape(bd, di, N),
         w_out,
+        )
     )
     mixed = out if fused else lax.psum(out, "heads").astype(BF16)
     return (mixed, new_state.reshape(bd, hd, P_SIZE, N))

time: 47.7 us -> 39.5 us (0.83)
  local copies, waits for them, and re-layouts: 12.1 us -> 4.03 us
    unnamed x19 -> x2, local copies, waits for them, and re-layouts: 12.1 us -> 4.03 us
where the time goes in v2:
time: 39.5 us; the launch traced here: 39.3 us
  Pallas kernels  34.7 us (88%)
  local copies, waits for them, and re-layouts  4.03 us (10%)
  between operations  0.64 us (2%)
    pallas_call x1, Pallas kernels, on_device(): pl.pallas_call(functools.partial(kernel, dims), out_shape=(jax.ShapeDtype...  34.7 us
    unnamed x2, local copies, waits for them, and re-layouts  4.03 us

profile of v2, /device:TPU:0, one launch (start us, length us, event | category | flops | bytes accessed | tf_op | source)
XLA Modules:
  0.0 39.3 jit_solution(7105670060664572757)
XLA Ops:
  0.6 34.7 %shard_map.158 = (bf16[16,2048]{1,0:T(8,128)(2,1)S(1)}, f32[4,2048,256]{2,1,0:T(8,128)S(1)}) custom-call(bf16[16,2048]{1,0:T(8,128)(2,1)} %hidden_hbm.1, f32[1,32]{1,0:T(1,128)} %bitcast.15, f32[1,32]{1,0:T(1,128)} %bitcast.16, f32[1,32]{1,0:T(1,128)} %bitcast.17, bf16[3,4,2048]{2,1,0:T(4,128)(2,1)} %bitcast.13, f32[4,2048]{1,0:T(4,128)} %convwx_hbm.1, ...), custom_call_target="tpu_custom_call" | custom-call | tf_op jit(solution)/shard_map/pallas_call | solution.py:422
  35.3 3.4 %copy.19 = f32[4,32,64,256]{3,2,1,0:T(8,128)} copy(f32[4,32,64,256]{3,2,1,0:T(8,128)S(1)} %bitcast.9) | data formatting | bytes 16777216
  38.7 0.6 %copy.20 = bf16[16,2048]{1,0:T(8,128)(2,1)} copy(bf16[16,2048]{1,0:T(8,128)(2,1)S(1)} %get-tuple-element.10) | data formatting | bytes 131072

commit v3 on v2

--- a/solution.py
+++ b/solution.py
@@ -103,8 +103,14 @@
     def emb_peer(o):
         return lax.rem(e + o, n_emb)
 
-    def head_peer(o):
-        return lax.rem(h + o, n_heads)
+    def head_peer(mask):
+        peer = h
+        bit = 1
+        while bit < n_heads:
+            if mask & bit:
+                peer = peer + bit * (1 - 2 * lax.rem(lax.div(h, bit), 2))
+            bit *= 2
+        return peer
 
     copies = {}
     order = []
@@ -133,11 +139,13 @@
         stream(("x", c), wx_hbm.at[:, pl.ds(c * chunk, chunk)], wx_v.at[c])
     for c in range(n_chunk):
         stream(("z", c), wz_hbm.at[:, pl.ds(c * chunk, chunk)], wz_v.at[c])
-    for b in range(bd):
-        stream(("s", b), state_hbm.at[b], st_ref.at[b])
+    rows_in = min(512, di)
+    for i in range(di // rows_in):
+        part = pl.ds(i * rows_in, rows_in)
+        stream(("s", i), state_hbm.at[:, part], st_ref.at[:, part])
     n_out = cols // ochunk
     for i in range(n_out):
-        at = lax.rem(h + i + 1, n_heads) if fused else i
+        at = head_peer(n_heads - 1 - i) if fused else i
         off = pl.multiple_of(at * ochunk, ochunk)
         stream(("o", i), wout_hbm.at[:, pl.ds(off, ochunk)], wout_v.at[i])
     started = [0]
@@ -264,31 +272,37 @@
     c_high, c_low, _ = split3(c_group)
     c_both = jnp.concatenate([c_high.astype(F32), c_low.astype(F32)], axis=0).astype(BF16)
 
-    rows_at = 256 if di % 256 == 0 else di
-    for b in range(bd):
-        ready(("s", b))
-        b_row = b_group[b : b + 1, :]
-
-        def update(i, carry, b=b, b_row=b_row):
-            at = pl.ds(pl.multiple_of(i * rows_at, rows_at), rows_at)
-            xcol = cols_v[at, b : b + 1]
-            dcol = cols_v[at, bd + b : bd + b + 1]
-            new = dcol * st_ref[b, at, :] + xcol * b_row
-            st_ref[b, at, :] = new
-            got = lax.dot_general(
-                c_both, new.astype(BF16), (((1,), (1,)), ((), ())), preferred_element_type=F32
-            )
-            read_v[b : b + 1, at] = got[b : b + 1, :] + got[bd + b : bd + b + 1, :]
+    rows_at = min(256, rows_in)
+    lane = lax.broadcasted_iota(jnp.int32, (rows_at, 2 * bd), 1)
+    for i in range(di // rows_in):
+        ready(("s", i))
+
+        def update(j, carry, i=i):
+            at = pl.ds(pl.multiple_of(i * rows_in + j * rows_at, rows_at), rows_at)
+            found = None
+            for b in range(bd):
+                xcol = cols_v[at, b : b + 1]
+                dcol = cols_v[at, bd + b : bd + b + 1]
+                new = dcol * st_ref[b, at, :] + xcol * b_group[b : b + 1, :]
+                st_ref[b, at, :] = new
+                got = lax.dot_general(
+                    new.astype(BF16), c_both, (((1,), (1,)), ((), ())), preferred_element_type=F32
+                )
+                mine = (lane == b) | (lane == bd + b)
+                found = got if found is None else jnp.where(mine, got, found)
+            read_v[at, :] = found
             return carry
 
-        lax.fori_loop(0, di // rows_at, update, 0)
+        lax.fori_loop(0, rows_in // rows_at, update, 0)
+    read_rows = jnp.transpose(read_v[...])
+    read = read_rows[0:bd] + read_rows[bd : 2 * bd]
 
     for copy in z_copies:
         copy.wait_recv()
     zall = zsend[e]
     for o in range(n_emb - 1):
         zall = zall + zrecv[o]
-    gated = (read_v[...] + xc_v[...]) * silu(zall)
+    gated = (read + xc_v[...]) * silu(zall)
     total = jnp.sum(gated * gated, axis=1, keepdims=True)
     q_copies = []
     if span > 1:
@@ -340,7 +354,7 @@
                 dst_ref=rs_recv.at[i],
                 send_sem=r_ss.at[i],
                 recv_sem=r_rs.at[i],
-                device_id={"heads": head_peer(i + 1)},
+                device_id={"heads": head_peer(n_heads - 1 - i)},
                 device_id_type=MESH,
             )
             copy.start()
@@ -353,7 +367,7 @@
             copy.wait_recv()
             own = own + rs_recv[i].astype(F32)
         fin_send[...] = own.astype(BF16)
-        for o in range(1, n_heads):
+        for o in range(n_heads - 1, 0, -1):
             copy = pltpu.make_async_remote_copy(
                 src_ref=fin_send,
                 dst_ref=fin_v.at[h],
@@ -410,7 +424,7 @@
     n_chunk = di // chunk
     n_out = cols // ochunk
     x_cols = di + 2 * N + LANES
-    n_streams = 14 + 2 * n_chunk + bd + n_out
+    n_streams = 14 + 2 * n_chunk + di // min(512, di) + n_out
     vm = pl.BlockSpec(memory_space=pltpu.VMEM)
     hbm = pl.BlockSpec(memory_space=pltpu.HBM)
     dma = pltpu.SemaphoreType.DMA
@@ -447,7 +461,7 @@
             pltpu.VMEM((n_emb, bd, di), F32),
             pltpu.VMEM((e_n, bd, di), F32),
             pltpu.VMEM((di, 2 * bd), F32),
-            pltpu.VMEM((bd, di), F32),
+            pltpu.VMEM((di, 2 * bd), F32),
             pltpu.VMEM((bd, di), F32),
             pltpu.VMEM((n_emb, bd, di), BF16),
             pltpu.VMEM((rs_n,) + rs_shape, BF16),

time: 39.5 us -> 34.8 us (0.88)
  Pallas kernels: 34.7 us -> 29.9 us
    pallas_call x1, Pallas kernels: 34.7 us -> 29.9 us  [on_device(): pl.pallas_call(functools.partial(kernel, dims), out_shape=(jax.ShapeDtype...]
where the time goes in v3:
time: 34.8 us; the launch traced here: 34.6 us
  Pallas kernels  29.9 us (86%)
  local copies, waits for them, and re-layouts  4.03 us (12%)
  between operations  0.64 us (2%)
    pallas_call x1, Pallas kernels, on_device(): pl.pallas_call(functools.partial(kernel, dims), out_shape=(jax.ShapeDtype...  29.9 us
    unnamed x2, local copies, waits for them, and re-layouts  4.03 us

profile of v3, /device:TPU:0, one launch (start us, length us, event | category | flops | bytes accessed | tf_op | source)
XLA Modules:
  0.0 34.6 jit_solution(17921242407619379135)
XLA Ops:
  0.6 29.9 %shard_map.158 = (bf16[16,2048]{1,0:T(8,128)(2,1)S(1)}, f32[4,2048,256]{2,1,0:T(8,128)S(1)}) custom-call(bf16[16,2048]{1,0:T(8,128)(2,1)} %hidden_hbm.1, f32[1,32]{1,0:T(1,128)} %bitcast.15, f32[1,32]{1,0:T(1,128)} %bitcast.16, f32[1,32]{1,0:T(1,128)} %bitcast.17, bf16[3,4,2048]{2,1,0:T(4,128)(2,1)} %bitcast.13, f32[4,2048]{1,0:T(4,128)} %convwx_hbm.1, ...), custom_call_target="tpu_custom_call" | custom-call | tf_op jit(solution)/shard_map/pallas_call | solution.py:436
  30.6 3.4 %copy.19 = f32[4,32,64,256]{3,2,1,0:T(8,128)} copy(f32[4,32,64,256]{3,2,1,0:T(8,128)S(1)} %bitcast.9) | data formatting | bytes 16777216
  34.0 0.6 %copy.20 = bf16[16,2048]{1,0:T(8,128)(2,1)} copy(bf16[16,2048]{1,0:T(8,128)(2,1)S(1)} %get-tuple-element.10) | data formatting | bytes 131072

commit v4 on v3

--- a/solution.py
+++ b/solution.py
@@ -157,7 +157,8 @@
 
     def ready(name):
         copies[name].wait()
-        advance()
+        if name[0] in ("bc", "x", "z", "s", "o"):
+            advance()
 
     for _ in range(DEPTH + 12):
         advance()

time: 34.8 us -> 34.8 us (level)
  no operation moved by 1% of the time
where the time goes in v4:
time: 34.8 us; the launch traced here: 34.6 us
  Pallas kernels  29.9 us (86%)
  local copies, waits for them, and re-layouts  4.03 us (12%)
  between operations  0.64 us (2%)
    pallas_call x1, Pallas kernels, on_device(): pl.pallas_call(functools.partial(kernel, dims), out_shape=(jax.ShapeDtype...  29.9 us
    unnamed x2, local copies, waits for them, and re-layouts  4.03 us

profile of v4, /device:TPU:0, one launch (start us, length us, event | category | flops | bytes accessed | tf_op | source)
XLA Modules:
  0.0 34.6 jit_solution(7001315208149028297)
XLA Ops:
  0.6 29.9 %shard_map.158 = (bf16[16,2048]{1,0:T(8,128)(2,1)S(1)}, f32[4,2048,256]{2,1,0:T(8,128)S(1)}) custom-call(bf16[16,2048]{1,0:T(8,128)(2,1)} %hidden_hbm.1, f32[1,32]{1,0:T(1,128)} %bitcast.15, f32[1,32]{1,0:T(1,128)} %bitcast.16, f32[1,32]{1,0:T(1,128)} %bitcast.17, bf16[3,4,2048]{2,1,0:T(4,128)(2,1)} %bitcast.13, f32[4,2048]{1,0:T(4,128)} %convwx_hbm.1, ...), custom_call_target="tpu_custom_call" | custom-call | tf_op jit(solution)/shard_map/pallas_call | solution.py:437
  30.6 3.4 %copy.19 = f32[4,32,64,256]{3,2,1,0:T(8,128)} copy(f32[4,32,64,256]{3,2,1,0:T(8,128)S(1)} %bitcast.9) | data formatting | bytes 16777216
  34.0 0.6 %copy.20 = bf16[16,2048]{1,0:T(8,128)(2,1)} copy(bf16[16,2048]{1,0:T(8,128)(2,1)S(1)} %get-tuple-element.10) | data formatting | bytes 131072
